TPU v7x, 32 devices: a whole 2x2x4 slice. The times are simulated.
32 devices in a mesh: freq: 8 (over z, y), rows: 4 (over x, core).
Axes of the slice: x: 2, y: 2, z: 4, core: 2. Of those that a mesh axis runs over, the one named last changes fastest.
Arguments:
- wavefield: bfloat16 [10240, 32, 1024], P('freq', 'rows'), may hold values from -6 to 6
- u_factors: bfloat16 [2, 16, 4, 256, 512], P(None, 'freq', 'rows'), may hold values from -0.25 to 0.25
- v_factors: bfloat16 [2, 16, 4, 512, 256], P(None, 'freq', 'rows'), may hold values from -0.375 to 0.375
- tile_ranks: int32 [16, 4, 40], P('freq', 'rows'), may hold values from 1 to 64, as said below
- tile_offsets: int32 [16, 4, 40], P('freq', 'rows'), may hold values from 0 to 511, as said below
Outputs:
- convolved: bfloat16 [1024, 32, 1024], P(('rows', 'freq'))
Inputs may be any that keep to these rules, and one draw needn't show every extreme that they name: tile_ranks[k, i, j] is the rank of tile (i, j) of frequency k; the ranks of one tile row sum to at most 512, exactly 512 on some row of every draw, and every tile row has a tile of rank 64. tile_offsets[k, i, j] is the sum of tile_ranks[k, i, j2] over j2 < j.
All inputs are finite; a program needn't handle non-finite values.
Results may differ from a plain program's by a relative error of at most 0.0072.
Values may be sent and summed in bfloat16 or wider, within the bound.
A program may use at most 128 MiB of HBM per device.

v0:
```python
import functools
import math
import jax
import jax.numpy as jnp
from jax import lax
from jax.sharding import PartitionSpec as P

RANK_MAX = 64


def spectral_tables(freq_count, sample_count):
    freq_bins = jnp.arange(freq_count, dtype=jnp.int32) + 1
    sample_index = jnp.arange(sample_count, dtype=jnp.int32)
    phase_int = freq_bins[:, None] * sample_index[None, :] % sample_count
    angles = phase_int.astype(jnp.float32) * (2.0 * math.pi / sample_count)
    cosine = jnp.cos(angles)
    minus_sine = -jnp.sin(angles)
    stacked = jnp.stack([cosine, minus_sine], axis=1)
    forward = (stacked / math.sqrt(sample_count)).astype(jnp.bfloat16)
    inverse = (stacked / math.sqrt(freq_count)).astype(jnp.bfloat16)
    return (forward, inverse)


def tile_windows(v_row, u_row, starts, rank_max):
    columns = starts.shape[0]
    slot_index = (starts[:, None] + jnp.arange(rank_max, dtype=jnp.int32)[None, :]).reshape(-1)
    v_padded = jnp.pad(v_row, ((0, 0), (0, rank_max), (0, 0)))
    u_padded = jnp.pad(u_row, ((0, 0), (0, 0), (0, rank_max)))
    v_win = jnp.take(v_padded, slot_index, axis=1).reshape(2, columns, rank_max, v_row.shape[2])
    u_win = jnp.take(u_padded, slot_index, axis=2).reshape(2, u_row.shape[1], columns, rank_max)
    return (v_win, u_win)


def slot_lookup(starts, counts, rank_max, slot_count):
    position = jnp.arange(slot_count, dtype=jnp.int32)
    started = starts[:, None, :] <= position[None, :, None]
    owner_tile = jnp.sum(started.astype(jnp.int32), axis=2) - 1
    first_slot = jnp.max(jnp.where(started, starts[:, None, :], 0), axis=2)
    within = position[None, :] - first_slot
    live_slot = position[None, :] < (starts[:, -1] + counts[:, -1])[:, None]
    flat_index = jnp.where(live_slot, owner_tile * rank_max + within, 0)
    return (flat_index, live_slot)


def take_slots(values, chosen):
    return jnp.take(values, chosen, axis=1)


def per_device(wavefield, u_factors, v_factors, tile_ranks, tile_offsets):
    rec_dev, src_dev, samples = wavefield.shape
    freq_dev = u_factors.shape[1]
    rows_dev = u_factors.shape[2]
    tile_size = u_factors.shape[3]
    slot_count = u_factors.shape[4]
    freq_group = lax.axis_size("freq")
    row_group = lax.axis_size("rows")
    freqs = freq_dev * freq_group
    receivers = rec_dev * freq_group
    columns = receivers // tile_size
    sources = src_dev * row_group
    forward, inverse = spectral_tables(freqs, samples)
    spectrum = jnp.einsum("kct,rst->kcrs", forward, wavefield, preferred_element_type=jnp.float32)
    spectrum = spectrum.astype(jnp.bfloat16).reshape(freqs, 2, rec_dev * src_dev)
    windows = jax.vmap(
        functools.partial(tile_windows, rank_max=RANK_MAX), in_axes=(1, 1, 0), out_axes=(1, 1)
    )
    rank_slots = jnp.arange(RANK_MAX, dtype=jnp.int32)
    tile_row = 0
    v_win, u_win = windows(
        v_factors[:, :, tile_row], u_factors[:, :, tile_row], tile_offsets[:, tile_row]
    )
    rank_mask = rank_slots[None, None, :] < tile_ranks[:, tile_row, :, None]
    flat_index, live_slot = slot_lookup(
        tile_offsets[:, tile_row], tile_ranks[:, tile_row], RANK_MAX, slot_count
    )
    prepared = [(v_win, u_win, rank_mask, flat_index, live_slot)]
    by_frequency = lax.all_to_all(spectrum, "freq", split_axis=0, concat_axis=2, tiled=True)
    portion = lax.all_gather(by_frequency[None], "rows", axis=0, tiled=True)
    blocks_in = portion.shape[0]
    spectra = portion.reshape(blocks_in, freq_dev, 2, columns, tile_size, src_dev)
    spectra = jnp.transpose(spectra, (1, 2, 3, 4, 0, 5)).reshape(
        freq_dev, 2, columns, tile_size, blocks_in * src_dev
    )
    tile_row = 0
    v_win, u_win, rank_mask, flat_index, live_slot = prepared[tile_row]
    quadrants = jnp.einsum(
        "afjmr,fbjrs->fabjms", v_win, spectra, preferred_element_type=jnp.float32
    )
    coeffs = jnp.stack(
        [quadrants[:, 0, 0] - quadrants[:, 1, 1], quadrants[:, 0, 1] + quadrants[:, 1, 0]], axis=1
    )
    coeffs = jnp.where(rank_mask[:, None, :, :, None], coeffs, 0.0).astype(jnp.bfloat16)
    stacked = coeffs.reshape(freq_dev, 2, columns * RANK_MAX, blocks_in * src_dev)
    packed = jax.vmap(take_slots)(stacked, flat_index)
    packed = jnp.where(live_slot[:, None, :, None], packed, jnp.zeros((), jnp.bfloat16))
    products = jnp.einsum(
        "afrk,fcks->facrs", u_factors[:, :, tile_row], packed, preferred_element_type=jnp.float32
    )
    results = [
        jnp.stack(
            [products[:, 0, 0] - products[:, 1, 1], products[:, 0, 1] + products[:, 1, 0]], axis=1
        )
    ]
    merged = jnp.stack(results, axis=2)
    bands = merged.astype(jnp.bfloat16).reshape(
        freq_dev, 2, rows_dev * tile_size, blocks_in, src_dev
    )
    bands = bands.reshape(freq_dev, 2, rows_dev * tile_size * sources)
    returned = lax.all_to_all(bands, "freq", split_axis=2, concat_axis=0, tiled=True)
    series = jnp.einsum("kcq,kct->qt", returned, inverse, preferred_element_type=jnp.float32)
    return series.astype(jnp.bfloat16).reshape(rows_dev * tile_size // freq_group, sources, samples)


def solution(mesh):
    placed = (
        P("freq", "rows", None),
        P(None, "freq", "rows", None, None),
        P(None, "freq", "rows", None, None),
        P("freq", "rows", None),
        P("freq", "rows", None),
    )
    return jax.shard_map(
        per_device,
        mesh=mesh,
        in_specs=placed,
        out_specs=P(("rows", "freq"), None, None),
        check_vma=False,
    )
```

profile of v0, /device:TPU:0, one launch (start us, length us, event | category | flops | bytes accessed | tf_op | source)
XLA Modules:
  0.0 294.8 jit_solution(15557455718139508555)
XLA Ops:
  6.9 24.3 %fusion.6 = bf16[16,2,1280,8]{2,0,3,1:T(8,128)(2,1)S(1)} fusion(bf16[1280,8,1024]{2,1,0:T(8,128)(2,1)} %param.5, f32[16,1,1024]{2,0,1:T(8,128)S(1)} %get-tuple-element.14, f32[16,1,1024]{2,0,1:T(8,128)S(1)} %get-tuple-element.13), kind=kOutput, calls=%fused_computation.10 | convolution fusion | flops 671514624 | bytes 21757952 | tf_op jit(solution)/shard_map/kct,rst->kcrs/dot_general | solution.py:62
  31.2 4.5 %copy.92 = bf16[16,2,1280,8]{0,3,2,1:T(8,128)(2,1)} copy(bf16[16,2,1280,8]{2,0,3,1:T(8,128)(2,1)S(1)} %fusion.6) | data formatting | bytes 1310720 | tf_op jit(solution)/shard_map/convert_element_type | solution.py:63
  35.7 4.8 %copy.93 = bf16[16,2,10240]{2,1,0:T(2,128)(2,1)S(1)} copy(bf16[16,2,10240]{0,2,1:T(8,128)(2,1)} %bitcast.107) | data formatting | bytes 1310720 | tf_op jit(solution)/shard_map/reshape | solution.py:63
  40.5 24.9 %all_to_all.33 = bf16[16,2,10240]{2,1,0:T(2,128)(2,1)S(1)} all-to-all(bf16[16,2,10240]{2,1,0:T(2,128)(2,1)S(1)} %copy.93), channel_id=1, replica_groups=mesh['freq'=8,'rows'=4] {'freq'}, dimensions={0} | all-to-all | bytes 1310720 | tf_op jit(solution)/shard_map/all_to_all | solution.py:77
  65.8 1.2 broadcast_in_dim.78
  67.4 1.1 copy.141
  68.5 1.0 pad_bitcast_fusion
  69.5 45.7 %gather_fusion = bf16[5120,2,256]{2,1,0:T(2,128)(2,1)} fusion(bf16[2,2,576,256]{3,1,2,0:T(2,128)(2,1)S(1)} %pad_bitcast_fusion, s32[5120]{0:T(1024)S(1)} %reshape.407), kind=kCustom, calls=%fused_computation | custom fusion | bytes 10526720 | tf_op jit(solution)/shard_map/vmap(jit(_take))/gather | solution.py:29
  115.2 5.5 %copy.97 = bf16[2,2560,2,256]{3,1,2,0:T(8,128)(2,1)} copy(bf16[2,2560,2,256]{3,2,1,0:T(2,128)(2,1)} %bitcast.106) | data formatting | bytes 10485760 | tf_op jit(solution)/shard_map/vmap(jit(_take))/gather | solution.py:29
  121.5 74.5 %reshape.404 = bf16[4,2,2,40,256,8]{5,4,3,2,1,0:T(8,128)(2,1)} reshape(bf16[4,2,2,81920]{3,2,1,0:T(2,128)(2,1)} %all-gather.2.cloned.1.call-done) | data formatting | bytes 5242880 | tf_op jit(solution)/shard_map/reshape | solution.py:80
  196.0 30.3 %copy.95 = bf16[2,2,40,256,4,8]{3,5,4,1,2,0:T(8,128)(2,1)} copy(bf16[2,2,40,256,4,8]{5,3,2,1,0,4:T(8,128)(2,1)} %bitcast.104) | data formatting | bytes 5242880 | tf_op jit(solution)/shard_map/transpose | solution.py:81
  226.3 5.3 %fusion.9 = f32[2,2,2,40,64,32]{4,5,1,2,3,0:T(8,128)S(1)} fusion(bf16[2,2,40,256,4,8]{3,5,4,1,2,0:T(8,128)(2,1)} %copy.95, bf16[2,2,40,64,256]{4,3,2,1,0:T(8,128)(2,1)} %bitcast.110, pred[2,40,64]{2,1,0:T(8,128)(4,1)S(1)} %fusion.32), kind=kOutput, calls=%fused_computation.11 | convolution fusion | flops 338165760 | bytes 10490880 | tf_op jit(solution)/shard_map/afjmr,fbjrs->fabjms/dot_general | solution.py:86
  231.6 0.6 slice_subtract_fusion
  232.5 0.4 sub.52
  233.7 4.1 %copy.103 = bf16[2,2,2560,32]{3,1,2,0:T(2,128)(2,1)} copy(bf16[2,2,2560,32]{2,3,1,0:T(8,128)(2,1)S(1)} %fusion.14) | data formatting | bytes 1310720 | tf_op jit(solution)/shard_map/convert_element_type | solution.py:92
  237.7 6.2 %gather_fusion.1 = bf16[1024,2,32]{2,1,0:T(2,128)(2,1)S(1)} fusion(bf16[2,2,2560,32]{3,1,2,0:T(2,128)(2,1)} %copy.103, s32[1024]{0:T(1024)S(1)} %bitcast.105), kind=kCustom, calls=%fused_computation.1 | custom fusion | bytes 270336 | tf_op jit(solution)/shard_map/vmap(jit(_take))/gather | solution.py:46
  244.0 0.4 copy.119
  244.5 0.4 convolution_bitcast_fusion
  245.7 6.9 %copy.109 = bf16[2,2,8192]{0,1,2:T(2,128)(2,1)} copy(bf16[2,2,8192]{2,0,1:T(2,128)(2,1)S(1)} %pad_maximum_fusion.1) | data formatting | bytes 131072 | tf_op jit(solution)/shard_map/stack | solution.py:100
  252.6 7.2 %reshape.427 = bf16[8,2,2048]{2,1,0:T(2,128)(2,1)S(1)} reshape(bf16[8192,2,2]{2,1,0:T(2,128)(2,1)} %bitcast.108) | data formatting | bytes 131072
  259.7 10.0 %all_to_all.34 = bf16[8,2,2048]{2,1,0:T(2,128)(2,1)S(1)} all-to-all(bf16[8,2,2048]{2,1,0:T(2,128)(2,1)S(1)} %reshape.427), channel_id=1, replica_groups=mesh['freq'=8,'rows'=4] {'freq'}, dimensions={0} | all-to-all | bytes 131072 | tf_op jit(solution)/shard_map/all_to_all | solution.py:109
  269.7 10.0 %reshape.428 = bf16[8192,2,2]{2,1,0:T(2,128)(2,1)} reshape(bf16[8,2,2048]{2,1,0:T(2,128)(2,1)S(1)} %all_to_all.34) | data formatting | bytes 131072
  279.7 6.1 %copy.124 = bf16[2,2,8,1024]{3,2,1,0:T(8,128)(2,1)S(1)} copy(bf16[2,2,8,1024]{0,1,3,2:T(2,128)(2,1)} %bitcast.109) | data formatting | bytes 131072 | tf_op jit(solution)/shard_map/all_to_all | solution.py:109
  285.9 2.0 bitcast_convert_fusion
  (42 shorter events, 3.8 us)
Async XLA Ops:
  6.5 238.0 %copy-start = (bf16[2,2,1,256,512]{4,3,2,1,0:T(8,128)(2,1)S(1)}, bf16[2,2,1,256,512]{4,3,2,1,0:T(8,128)(2,1)}, u32[]{:S(2)}) copy-start(bf16[2,2,1,256,512]{4,3,2,1,0:T(8,128)(2,1)} %param.6) | copy-start | bytes 3145732
  6.5 115.0 %all-gather.2.cloned.1.call-start = ((), (), s32[]{:S(2)}) async-start(), calls=%async_computation.2 | async-start | bytes 3276800 | tf_op jit(solution)/shard_map/all_gather | solution.py:78
  40.5 26.6 %copy-start.2 = (s32[2,1,40]{2,1,0:T(1,128)S(1)}, s32[2,1,40]{2,1,0:T(1,128)}, u32[]{:S(2)}) copy-start(s32[2,1,40]{2,1,0:T(1,128)} %param.9) | copy-start | bytes 964
  40.5 26.9 %copy-start.1 = (bf16[2,2,1,512,256]{4,3,2,1,0:T(8,128)(2,1)S(1)}, bf16[2,2,1,512,256]{4,3,2,1,0:T(8,128)(2,1)}, u32[]{:S(2)}) copy-start(bf16[2,2,1,512,256]{4,3,2,1,0:T(8,128)(2,1)} %param.7) | copy-start | bytes 3145732
  115.2 5.5 %copy-start.3 = (s32[2,1,40]{2,1,0:T(1,128)S(1)}, s32[2,1,40]{2,1,0:T(1,128)}, u32[]{:S(2)}) copy-start(s32[2,1,40]{2,1,0:T(1,128)} %param.8) | copy-start | bytes 964
Sparse Core Ops, SparseCore 0:
  67.2 24.1 all-gather.1
where the time goes:
time: 296 us; the launch traced here: 295 us
  local copies, waits for them, and re-layouts  212 us (72%)
  blocking collectives  34.9 us (12%)
  matrix products  32.1 us (11%)
  between operations  13.7 us (5%)
    reshape x1, local copies, waits for them, and re-layouts, per_device(): portion.reshape(blocks_in, freq_dev, 2, columns, tile_size, src_dev)  74.5 us
    gather x3, local copies, waits for them, and re-layouts, tile_windows(): jnp.take(v_padded, slot_index, axis=1)  51.3 us
    transpose x1, local copies, waits for them, and re-layouts, per_device(): jnp.transpose(spectra, (1, 2, 3, 4, 0, 5))  30.3 us
    all_to_all x1, blocking collectives, per_device(): lax.all_to_all(spectrum, 'freq', split_axis=0, concat_axis=2, tiled=True)  24.9 us
    dot_general x1, matrix products, per_device(): jnp.einsum('kct,rst->kcrs', forward, wavefield, preferred_element_type=jn...  24.3 us
    unnamed x12, local copies, waits for them, and re-layouts  18.3 us
    all_to_all x1, blocking collectives, per_device(): lax.all_to_all(bands, 'freq', split_axis=2, concat_axis=0, tiled=True)  9.96 us
    another operation x1, local copies, waits for them, and re-layouts, per_device(): jnp.stack([products[:, 0, 0] - products[:, 1, 1], products[:, 0, 1] + pro...  6.87 us
  transfers between devices with their start and end apart: 1, of which 0 were waited for; matrix products, arithmetic and copies ran while one was open for 18% of the time, Pallas kernels for 0%

commit v1 on v0

--- a/solution.py
+++ b/solution.py
@@ -106,7 +106,10 @@
         freq_dev, 2, rows_dev * tile_size, blocks_in, src_dev
     )
     bands = bands.reshape(freq_dev, 2, rows_dev * tile_size * sources)
-    returned = lax.all_to_all(bands, "freq", split_axis=2, concat_axis=0, tiled=True)
+    returned = jnp.concatenate(
+        lax.all_to_all(jnp.stack(jnp.split(bands, lax.axis_size("freq"), axis=2)), "freq", 0, 0),
+        axis=0,
+    )
     series = jnp.einsum("kcq,kct->qt", returned, inverse, preferred_element_type=jnp.float32)
     return series.astype(jnp.bfloat16).reshape(rows_dev * tile_size // freq_group, sources, samples)
 

time: 296 us -> 266 us (0.90)
  local copies, waits for them, and re-layouts: 212 us -> 182 us
    unnamed x12 -> x18, local copies, waits for them, and re-layouts: 18.3 us -> 1.23 us
    another operation x1, local copies, waits for them, and re-layouts: 6.87 us -> 0.04 us  [per_device(): jnp.stack([products[:, 0, 0] - products[:, 1, 1], products[:, 0, 1] + pro...]
    all_to_all x3 -> x1, local copies, waits for them, and re-layouts: 6.2 us -> 0.05 us  [per_device(): lax.all_to_all(jnp.stack(jnp.split(bands, lax.axis_size('freq'), axis=2))...]
  transfers between devices with their start and end apart: 1 -> 1, of which waited for: 0 -> 0; matrix products, arithmetic and copies ran while one was open for 18% -> 21% of each run, Pallas kernels for 0% -> 0%
where the time goes in v1:
time: 266 us; the launch traced here: 265 us
  local copies, waits for them, and re-layouts  182 us (68%)
  blocking collectives  34.9 us (13%)
  matrix products  32.1 us (12%)
  between operations  13.7 us (5%)
    reshape x1, local copies, waits for them, and re-layouts, per_device(): portion.reshape(blocks_in, freq_dev, 2, columns, tile_size, src_dev)  74.5 us
    gather x3, local copies, waits for them, and re-layouts, tile_windows(): jnp.take(v_padded, slot_index, axis=1)  51.3 us
    transpose x1, local copies, waits for them, and re-layouts, per_device(): jnp.transpose(spectra, (1, 2, 3, 4, 0, 5))  30.3 us
    all_to_all x1, blocking collectives, per_device(): lax.all_to_all(spectrum, 'freq', split_axis=0, concat_axis=2, tiled=True)  24.9 us
    dot_general x1, matrix products, per_device(): jnp.einsum('kct,rst->kcrs', forward, wavefield, preferred_element_type=jn...  24.3 us
    all_to_all x1, blocking collectives, per_device(): lax.all_to_all(jnp.stack(jnp.split(bands, lax.axis_size('freq'), axis=2))...  9.96 us
    gather x2, local copies, waits for them, and re-layouts, take_slots(): return jnp.take(values, chosen, axis=1)  6.61 us
  transfers between devices with their start and end apart: 1, of which 0 were waited for; matrix products, arithmetic and copies ran while one was open for 21% of the time, Pallas kernels for 0%

profile of v1, /device:TPU:0, one launch (start us, length us, event | category | flops | bytes accessed | tf_op | source)
XLA Modules:
  0.0 264.7 jit_solution(9265371008938984903)
XLA Ops:
  6.5 0.3 fusion.33
  6.9 24.3 %fusion.6 = bf16[16,2,1280,8]{2,0,3,1:T(8,128)(2,1)S(1)} fusion(bf16[1280,8,1024]{2,1,0:T(8,128)(2,1)} %param.5, f32[16,1,1024]{2,0,1:T(8,128)S(1)} %get-tuple-element.14, f32[16,1,1024]{2,0,1:T(8,128)S(1)} %get-tuple-element.13), kind=kOutput, calls=%fused_computation.10 | convolution fusion | flops 671514624 | bytes 21757952 | tf_op jit(solution)/shard_map/kct,rst->kcrs/dot_general | solution.py:62
  31.2 4.5 %copy.93 = bf16[16,2,1280,8]{0,3,2,1:T(8,128)(2,1)} copy(bf16[16,2,1280,8]{2,0,3,1:T(8,128)(2,1)S(1)} %fusion.6) | data formatting | bytes 1310720 | tf_op jit(solution)/shard_map/convert_element_type | solution.py:63
  35.7 4.8 %copy.94 = bf16[16,2,10240]{2,1,0:T(2,128)(2,1)S(1)} copy(bf16[16,2,10240]{0,2,1:T(8,128)(2,1)} %bitcast.135) | data formatting | bytes 1310720 | tf_op jit(solution)/shard_map/reshape | solution.py:63
  40.5 24.9 %all_to_all.20 = bf16[16,2,10240]{2,1,0:T(2,128)(2,1)S(1)} all-to-all(bf16[16,2,10240]{2,1,0:T(2,128)(2,1)S(1)} %copy.94), channel_id=1, replica_groups=mesh['freq'=8,'rows'=4] {'freq'}, dimensions={0} | all-to-all | bytes 1310720 | tf_op jit(solution)/shard_map/all_to_all | solution.py:77
  65.5 0.4 copy.95
  65.8 1.2 broadcast_in_dim.78
  67.4 1.1 copy.139
  68.5 1.0 pad_bitcast_fusion
  69.5 45.7 %gather_fusion = bf16[5120,2,256]{2,1,0:T(2,128)(2,1)} fusion(bf16[2,2,576,256]{3,1,2,0:T(2,128)(2,1)S(1)} %pad_bitcast_fusion, s32[5120]{0:T(1024)S(1)} %reshape.411), kind=kCustom, calls=%fused_computation | custom fusion | bytes 10526720 | tf_op jit(solution)/shard_map/vmap(jit(_take))/gather | solution.py:29
  115.2 5.5 %copy.98 = bf16[2,2560,2,256]{3,1,2,0:T(8,128)(2,1)} copy(bf16[2,2560,2,256]{3,2,1,0:T(2,128)(2,1)} %bitcast.134) | data formatting | bytes 10485760 | tf_op jit(solution)/shard_map/vmap(jit(_take))/gather | solution.py:29
  121.5 74.5 %reshape.407 = bf16[4,2,2,40,256,8]{5,4,3,2,1,0:T(8,128)(2,1)} reshape(bf16[4,2,2,81920]{3,2,1,0:T(2,128)(2,1)} %all-gather.2.cloned.1.call-done) | data formatting | bytes 5242880 | tf_op jit(solution)/shard_map/reshape | solution.py:80
  196.0 30.3 %copy.96 = bf16[2,2,40,256,4,8]{3,5,4,1,2,0:T(8,128)(2,1)} copy(bf16[2,2,40,256,4,8]{5,3,2,1,0,4:T(8,128)(2,1)} %bitcast.132) | data formatting | bytes 5242880 | tf_op jit(solution)/shard_map/transpose | solution.py:81
  226.3 5.3 %fusion.9 = f32[2,2,2,40,64,32]{4,5,1,2,3,0:T(8,128)S(1)} fusion(bf16[2,2,40,256,4,8]{3,5,4,1,2,0:T(8,128)(2,1)} %copy.96, bf16[2,2,40,64,256]{4,3,2,1,0:T(8,128)(2,1)} %bitcast.136, pred[2,40,64]{2,1,0:T(8,128)(4,1)S(1)} %fusion.32), kind=kOutput, calls=%fused_computation.11 | convolution fusion | flops 338165760 | bytes 10490880 | tf_op jit(solution)/shard_map/afjmr,fbjrs->fabjms/dot_general | solution.py:86
  231.6 0.6 slice_subtract_fusion
  232.2 0.3 copy.100
  232.5 0.4 sub.52
  233.2 0.4 add.171
  233.7 4.1 %copy.104 = bf16[2,2,2560,32]{3,1,2,0:T(2,128)(2,1)} copy(bf16[2,2,2560,32]{2,3,1,0:T(8,128)(2,1)S(1)} %fusion.14) | data formatting | bytes 1310720 | tf_op jit(solution)/shard_map/convert_element_type | solution.py:92
  237.7 6.2 %gather_fusion.1 = bf16[1024,2,32]{2,1,0:T(2,128)(2,1)S(1)} fusion(bf16[2,2,2560,32]{3,1,2,0:T(2,128)(2,1)} %copy.104, s32[1024]{0:T(1024)S(1)} %bitcast.133), kind=kCustom, calls=%fused_computation.1 | custom fusion | bytes 270336 | tf_op jit(solution)/shard_map/vmap(jit(_take))/gather | solution.py:46
  244.0 0.4 copy.118
  244.5 0.4 convolution_bitcast_fusion
  245.8 10.0 %all_to_all.21 = bf16[8,2,2,1024]{3,1,2,0:T(2,128)(2,1)S(1)} all-to-all(bf16[8,2,2,1024]{3,1,2,0:T(2,128)(2,1)S(1)} %constant_dynamic-update-slice_fusion.2), channel_id=1, replica_groups=mesh['freq'=8,'rows'=4] {'freq'}, dimensions={0} | all-to-all | bytes 131072 | tf_op jit(solution)/shard_map/all_to_all | solution.py:110
  255.8 2.0 bitcast_convert_fusion
  (47 shorter events, 2.5 us)
Async XLA Ops:
  6.5 238.0 %copy-start = (bf16[2,2,1,256,512]{4,3,2,1,0:T(8,128)(2,1)S(1)}, bf16[2,2,1,256,512]{4,3,2,1,0:T(8,128)(2,1)}, u32[]{:S(2)}) copy-start(bf16[2,2,1,256,512]{4,3,2,1,0:T(8,128)(2,1)} %param.6) | copy-start | bytes 3145732
  6.5 115.0 %all-gather.2.cloned.1.call-start = ((), (), s32[]{:S(2)}) async-start(), calls=%async_computation.2 | async-start | bytes 3276800 | tf_op jit(solution)/shard_map/all_gather | solution.py:78
  40.5 26.6 %copy-start.2 = (s32[2,1,40]{2,1,0:T(1,128)S(1)}, s32[2,1,40]{2,1,0:T(1,128)}, u32[]{:S(2)}) copy-start(s32[2,1,40]{2,1,0:T(1,128)} %param.9) | copy-start | bytes 964
  40.5 26.9 %copy-start.1 = (bf16[2,2,1,512,256]{4,3,2,1,0:T(8,128)(2,1)S(1)}, bf16[2,2,1,512,256]{4,3,2,1,0:T(8,128)(2,1)}, u32[]{:S(2)}) copy-start(bf16[2,2,1,512,256]{4,3,2,1,0:T(8,128)(2,1)} %param.7) | copy-start | bytes 3145732
  115.2 5.5 %copy-start.3 = (s32[2,1,40]{2,1,0:T(1,128)S(1)}, s32[2,1,40]{2,1,0:T(1,128)}, u32[]{:S(2)}) copy-start(s32[2,1,40]{2,1,0:T(1,128)} %param.8) | copy-start | bytes 964
Sparse Core Ops, SparseCore 0:
  67.2 24.1 all-gather.1
